TPU v7x, 32 devices: a whole 2x2x4 slice. The times are simulated.
32 devices in a mesh: wide: 8 (over z, x), narrow: 4 (over y, core).
Axes of the slice: x: 2, y: 2, z: 4, core: 2. Of those that a mesh axis runs over, the one named last changes fastest.
Arguments:
- queries: bfloat16 [4096, 2048], P(('wide', 'narrow')), may hold values from -12 to 12
- keys: bfloat16 [4096, 2048], P(('wide', 'narrow')), may hold values from -24 to 24
- values: bfloat16 [4096, 2048], P(('wide', 'narrow')), may hold values from -6 to 6
- view_lengths: int32 [8, 4], P('wide'), may hold values from 1 to 256, 512 in all within a row
- gain: float32 [2048], replicated, may hold values from 0.25 to 1.75
- w_gate: bfloat16 [4, 512, 512], P('narrow', 'wide'), may hold values from -0.25 to 0.25
- w_up: bfloat16 [4, 512, 512], P('narrow', 'wide'), may hold values from -0.25 to 0.25
- w_down: bfloat16 [4, 512, 512], P('narrow', 'wide'), may hold values from -0.25 to 0.25
- m_gate: float32 [4, 512, 512], P('narrow', 'wide'), may hold values from -4 to 4
- m_up: float32 [4, 512, 512], P('narrow', 'wide'), may hold values from -4 to 4
- m_down: float32 [4, 512, 512], P('narrow', 'wide'), may hold values from -4 to 4
Outputs:
- output: bfloat16 [4096, 2048], P(('wide', 'narrow'))
- new_gate: bfloat16 [4, 512, 512], P('narrow', 'wide')
- new_up: bfloat16 [4, 512, 512], P('narrow', 'wide')
- new_down: bfloat16 [4, 512, 512], P('narrow', 'wide')
- mom_gate: float32 [4, 512, 512], P('narrow', 'wide')
- mom_up: float32 [4, 512, 512], P('narrow', 'wide')
- mom_down: float32 [4, 512, 512], P('narrow', 'wide')
Inputs may be any that keep to these rules, and one draw needn't show every extreme that they name: `view_lengths`: each row sums to 512; its largest entry is 256.
All inputs are finite; a program needn't handle non-finite values.
Results may differ from a plain program's by a relative error of at most 0.0091.
Values may be sent and summed in bfloat16 or wider, within the bound.
No kernel may reach another device: no remote copies, remote signals or barrier semaphores. Data moves between devices by JAX's collectives and lax.ppermute only.
A program may use at most 64 MiB of HBM per device.

v0:
```python
import jax
import jax.numpy as jnp
from jax import lax
from jax.sharding import PartitionSpec as P

momentum_decay = 0.9
step_size = 0.02
epsilon = 1e-06


def attend(query_rows, key_rows, value_rows, query_ids, key_ids):
    scaling = query_rows.shape[-1] ** (-0.5)
    scores = (
        jnp.einsum("rhd,ghd->hrg", query_rows, key_rows, preferred_element_type=jnp.float32)
        * scaling
    )
    allowed = query_ids[:, None] == key_ids[None, :]
    scores = jnp.where(allowed[None], scores, -1e30)
    highest = jnp.max(scores, axis=-1, keepdims=True)
    expo = jnp.exp(scores - highest)
    probs = (expo / jnp.sum(expo, axis=-1, keepdims=True)).astype(jnp.bfloat16)
    return jnp.einsum("hrg,ghd->rhd", probs, value_rows, preferred_element_type=jnp.float32)


def rms_gain(field, gains):
    return field * lax.rsqrt(jnp.mean(field * field, axis=-1, keepdims=True) + epsilon) * gains


def silu_slope(pre):
    sig = jax.nn.sigmoid(pre)
    return sig * (1.0 + pre * (1.0 - sig))


def block_gradients(key_rows, value_rows, gate_full, up_full, down_full):
    pre_gate = jnp.dot(key_rows, gate_full, preferred_element_type=jnp.float32)
    pre_up = jnp.dot(key_rows, up_full, preferred_element_type=jnp.float32)
    activ = jax.nn.silu(pre_gate)
    hidden = (activ * pre_up).astype(jnp.bfloat16)
    d_hidden = -lax.dot_general(
        value_rows, down_full, (((1,), (1,)), ((), ())), preferred_element_type=jnp.float32
    )
    d_gate = (d_hidden * pre_up * silu_slope(pre_gate)).astype(jnp.bfloat16)
    d_up = (d_hidden * activ).astype(jnp.bfloat16)
    contract = (((0,), (0,)), ((), ()))
    grad_gate = lax.dot_general(key_rows, d_gate, contract, preferred_element_type=jnp.float32)
    grad_up = lax.dot_general(key_rows, d_up, contract, preferred_element_type=jnp.float32)
    grad_down = -lax.dot_general(hidden, value_rows, contract, preferred_element_type=jnp.float32)
    return (grad_gate, grad_up, grad_down)


def gradients(key_rows, value_rows, gate_full, up_full, down_full):
    row_total, head_size = key_rows.shape
    block = min(row_total, 512)

    def add_block(number, totals):
        start = number * block
        terms = block_gradients(key_rows, value_rows, gate_full, up_full, down_full)
        return tuple((total + term for total, term in zip(totals, terms)))

    zeros = jnp.zeros((head_size, head_size), jnp.float32)
    return lax.fori_loop(0, row_total // block, add_block, (zeros, zeros, zeros))


def renormed(weight, moment, radius):
    old = weight.astype(jnp.float32)
    moved = old - step_size * moment / radius
    ratio = jnp.sqrt(jnp.sum(old * old, axis=-1, keepdims=True) + epsilon) / jnp.sqrt(
        jnp.sum(moved * moved, axis=-1, keepdims=True) + epsilon
    )
    return (moved * ratio).astype(jnp.bfloat16)


def apply_fast(query_rows, gate_full, up_full, down_full, gains):
    row_total, width = query_rows.shape
    block = min(row_total, 512)

    def one_block(block_rows):
        pre_gate = jnp.dot(block_rows, gate_full, preferred_element_type=jnp.float32)
        pre_up = jnp.dot(block_rows, up_full, preferred_element_type=jnp.float32)
        hidden = (jax.nn.silu(pre_gate) * pre_up).astype(jnp.bfloat16)
        fast_raw = jnp.dot(hidden, down_full, preferred_element_type=jnp.float32)
        return rms_gain(fast_raw, gains).astype(jnp.bfloat16)

    return lax.map(one_block, query_rows.reshape(row_total // block, block, width)).reshape(
        row_total, width
    )


def fast_branch(query_rows, key_rows, value_rows, gains, weights, moments):
    gate_full, up_full, down_full = (
        lax.all_gather(weights[0], "wide", axis=0, tiled=True),
        lax.all_gather(weights[1], "wide", axis=0, tiled=True),
        lax.all_gather(weights[2], "wide", axis=0, tiled=True),
    )
    grads = gradients(key_rows, value_rows, gate_full, up_full, down_full)
    wide_size = lax.axis_size("wide")
    grad_scale = float(key_rows.shape[0] * wide_size) ** (-0.5)
    head_size = key_rows.shape[1]
    row_count = weights[0].shape[0]
    offset = lax.axis_index("wide") * row_count
    blank = jnp.zeros((head_size, head_size), jnp.float32)
    placed = tuple(
        (
            lax.dynamic_update_slice_in_dim(blank, momentum_decay * moment, offset, 0)
            + part * grad_scale
            for moment, part in zip(moments, grads)
        )
    )
    full_moments = lax.psum(placed, "wide")
    full_new = tuple(
        (
            renormed(weight, moment, jnp.sqrt(jnp.mean(moment * moment) + epsilon))
            for weight, moment in zip((gate_full, up_full, down_full), full_moments)
        )
    )
    fresh = tuple((lax.dynamic_slice_in_dim(weight, offset, row_count, 0) for weight in full_new))
    moment_new = tuple(
        (lax.dynamic_slice_in_dim(moment, offset, row_count, 0) for moment in full_moments)
    )
    fast_out = apply_fast(query_rows, full_new[0], full_new[1], full_new[2], gains)
    return (fast_out, fresh, moment_new)


def per_device(
    queries, keys, values, view_lengths, gain, w_gate, w_up, w_down, m_gate, m_up, m_down
):
    narrow_size = lax.axis_size("narrow")
    narrow_index = lax.axis_index("narrow")
    tok_dev = queries.shape[0]
    group_size = tok_dev * narrow_size
    head_size = queries.shape[1] // narrow_size
    ends = jnp.cumsum(view_lengths[0])
    position = jnp.arange(group_size, dtype=jnp.int32)
    view_ids = jnp.sum((position[:, None] >= ends[None, :-1]).astype(jnp.int32), axis=1)
    head_gains = lax.dynamic_slice_in_dim(gain, narrow_index * head_size, head_size, 0)
    weights = (w_gate[0], w_up[0], w_down[0])
    moments = (m_gate[0], m_up[0], m_down[0])
    key_group, value_group = (
        lax.all_gather(keys, "narrow", axis=0, tiled=True),
        lax.all_gather(values, "narrow", axis=0, tiled=True),
    )
    own_ids = lax.dynamic_slice_in_dim(view_ids, narrow_index * tok_dev, tok_dev, 0)
    attn = attend(
        queries.reshape(tok_dev, narrow_size, head_size),
        key_group.reshape(group_size, narrow_size, head_size),
        value_group.reshape(group_size, narrow_size, head_size),
        own_ids,
        view_ids,
    )
    view_out = (
        rms_gain(attn, gain.reshape(narrow_size, head_size))
        .astype(jnp.bfloat16)
        .reshape(tok_dev, narrow_size * head_size)
    )
    query_head = lax.all_to_all(queries, "narrow", split_axis=1, concat_axis=0, tiled=True)
    key_head = lax.dynamic_slice_in_dim(key_group, narrow_index * head_size, head_size, 1)
    value_head = lax.dynamic_slice_in_dim(value_group, narrow_index * head_size, head_size, 1)
    fast_out, fresh, moment_new = fast_branch(
        query_head, key_head, value_head, head_gains, weights, moments
    )
    fast_tokens = lax.all_to_all(fast_out, "narrow", split_axis=0, concat_axis=1, tiled=True)
    output = (view_out.astype(jnp.float32) + fast_tokens.astype(jnp.float32)).astype(jnp.bfloat16)
    return (
        output,
        fresh[0][None],
        fresh[1][None],
        fresh[2][None],
        moment_new[0][None],
        moment_new[1][None],
        moment_new[2][None],
    )


def solution(mesh):
    in_specs = (
        P(("wide", "narrow"), None),
        P(("wide", "narrow"), None),
        P(("wide", "narrow"), None),
        P("wide", None),
        P(),
        P("narrow", "wide", None),
        P("narrow", "wide", None),
        P("narrow", "wide", None),
        P("narrow", "wide", None),
        P("narrow", "wide", None),
        P("narrow", "wide", None),
    )
    out_specs = (
        P(("wide", "narrow"), None),
        P("narrow", "wide", None),
        P("narrow", "wide", None),
        P("narrow", "wide", None),
        P("narrow", "wide", None),
        P("narrow", "wide", None),
        P("narrow", "wide", None),
    )
    return jax.shard_map(
        per_device, mesh=mesh, in_specs=in_specs, out_specs=out_specs, check_vma=False
    )
```

profile of v0, /device:TPU:0, one launch (start us, length us, event | category | flops | bytes accessed | tf_op | source)
XLA Modules:
  0.0 295.1 jit_solution(10100181000565378922)
XLA Ops:
  7.2 0.0 copy-start.17
  7.2 0.0 copy-start.18
  7.2 0.0 copy-start.19
  7.2 0.0 all-gather.6.cloned.1.call-start
  7.2 2.1 copy.39
  9.3 0.0 all-gather.6.cloned.1.call-update
  9.3 0.0 all-gather.8.cloned.1.call-start
  9.4 2.1 copy.42
  11.4 0.0 all-gather.8.cloned.1.call-update
  11.5 0.0 all-reduce.3.cloned.1.call-start
  11.5 0.0 copy-done.17
  11.5 33.2 %all-gather = bf16[1,512,512]{2,1,0:T(8,128)(2,1)S(1)} all-gather(bf16[1,64,512]{2,1,0:T(8,128)(2,1)S(1)} %copy-done.17), channel_id=2, replica_groups=mesh['wide'=8,'narrow'=4] {'wide'}, dimensions={1}, use_global_device_ids=true | all-gather | bytes 589824 | tf_op jit(solution)/shard_map/all_gather | solution.py:91
  44.7 0.0 copy-done.18
  44.7 31.4 %all-gather.2 = bf16[1,512,512]{2,1,0:T(8,128)(2,1)S(1)} all-gather(bf16[1,64,512]{2,1,0:T(8,128)(2,1)S(1)} %copy-done.18), channel_id=4, replica_groups=mesh['wide'=8,'narrow'=4] {'wide'}, dimensions={1}, use_global_device_ids=true | all-gather | bytes 589824 | tf_op jit(solution)/shard_map/all_gather | solution.py:92
  76.1 0.0 copy-done.19
  76.1 31.2 %all-gather.1 = bf16[1,512,512]{2,1,0:T(8,128)(2,1)S(1)} all-gather(bf16[1,64,512]{2,1,0:T(8,128)(2,1)S(1)} %copy-done.19), channel_id=3, replica_groups=mesh['wide'=8,'narrow'=4] {'wide'}, dimensions={1}, use_global_device_ids=true | all-gather | bytes 589824 | tf_op jit(solution)/shard_map/all_gather | solution.py:93
  107.3 2.5 fusion.21
  109.8 2.5 fusion.18
  112.3 1.7 convolution_negate_fusion.1
  114.0 0.1 copy-done.7
  114.1 2.4 convolution_multiply_fusion.1
  116.5 2.9 fusion.4
  119.4 0.0 copy-done.9
  119.4 1.6 convolution_multiply_fusion
  121.1 1.8 fusion.33
  122.9 0.0 all-reduce.3.cloned.1.call-update
  122.9 1.0 copy.38
  123.9 3.5 %all-to-all-start = ((bf16[128,4,512]{0,2,1:T(8,128)(2,1)}), bf16[128,4,512]{0,2,1:T(8,128)(2,1)S(1)}, u32[]{:S(2)}, u32[]{:S(2)}) async-start(bf16[128,4,512]{0,2,1:T(8,128)(2,1)} %bitcast.2), calls=%async_computation | async-start | bytes 1048576 | tf_op jit(solution)/shard_map/all_to_all | solution.py:155
  127.4 0.2 reduce-window.4
  127.6 0.0 copy-done.20
  127.6 0.1 dynamic_slice.36
  127.7 0.1 convert_reduce_fusion
  127.7 0.1 dynamic_slice.33
  127.8 0.1 broadcast_compare_fusion
  127.9 8.2 %all-to-all-done = bf16[128,4,512]{0,2,1:T(8,128)(2,1)S(1)} async-done(((bf16[128,4,512]{0,2,1:T(8,128)(2,1)}), bf16[128,4,512]{0,2,1:T(8,128)(2,1)S(1)}, u32[]{:S(2)}, u32[]{:S(2)}) %all-to-all-start) | async-done | bytes 524320 | tf_op jit(solution)/shard_map/all_to_all | solution.py:155
  136.2 1.0 copy.44
  137.2 2.6 fusion.5
  139.7 1.9 fusion.47
  141.6 4.4 %multiply_reduce_fusion.7 = (f32[128,4]{0,1:T(4,128)S(1)}, f32[128,4,512]{2,0,1:T(8,128)}) fusion(bf16[512,4,512]{0,2,1:T(8,128)(2,1)} %bitcast.95, f32[4,128]{1,0:T(4,128)S(1)} %fusion.47, f32[4,128,512]{2,1,0:T(8,128)} %fusion.5), kind=kOutput, calls=%fused_computation.49 | convolution fusion | flops 269746688 | bytes 4198400 | tf_op jit(solution)/shard_map/hrg,ghd->rhd/dot_general | solution.py:22
  146.0 107.3 %all-reduce.3.cloned.1.call-done = (f32[512,512]{1,0:T(8,128)}, f32[512,512]{1,0:T(8,128)}, f32[512,512]{1,0:T(8,128)}) async-done(((f32[512,512]{1,0:T(8,128)}, f32[512,512]{1,0:T(8,128)}, f32[512,512]{1,0:T(8,128)}), (f32[512,512]{1,0:T(8,128)}, f32[512,512]{1,0:T(8,128)}, f32[512,512]{1,0:T(8,128)})) %all-reduce.3.cloned.1.call-update) | async-done | bytes 3145744 | tf_op jit(solution)/shard_map/psum | solution.py:109
  253.2 2.2 multiply_reduce_fusion.6
  256.1 2.1 multiply_reduce_fusion.4
  258.9 0.9 multiply_reduce_fusion.2
  260.6 0.4 fusion.10
  261.0 1.0 multiply_convert_fusion.1
  262.0 1.5 fusion.9
  263.5 0.0 copy-done.6
  263.5 0.2 multiply_convert_fusion.3
  263.7 0.4 fusion.8
  264.1 0.2 multiply_convert_fusion.5
  264.3 0.6 dynamic-slice_bitcast_fusion.5
  264.9 0.6 dynamic-slice_bitcast_fusion.4
  265.6 1.5 convolution_bitcast_fusion.2
  267.1 3.4 %multiply_reduce_fusion = (f32[512]{0:T(512)S(1)}, f32[512,512]{1,0:T(8,128)}) fusion(bf16[512,512]{1,0:T(8,128)(2,1)} %multiply_convert_fusion.1, bf16[512,512]{1,0:T(8,128)(2,1)} %bitcast.93, bf16[512,512]{1,0:T(8,128)(2,1)} %copy-done.12, f32[512,512]{1,0:T(8,128)} %convolution_bitcast_fusion.2), kind=kOutput, calls=%fused_computation.28 | convolution fusion | flops 538967552 | bytes 3672064 | tf_op jit(solution)/shard_map/while/body/eval_jaxpr/dot_general | solution.py:81
  270.5 2.2 multiply_convert_fusion
  272.7 4.1 %all-to-all-start.1 = ((bf16[4,128,512]{2,1,0:T(8,128)(2,1)}), bf16[4,128,512]{2,1,0:T(8,128)(2,1)}, u32[]{:S(2)}, u32[]{:S(2)}) async-start(bf16[4,128,512]{2,1,0:T(8,128)(2,1)} %bitcast.90), calls=%async_computation.1 | async-start | bytes 1048576 | tf_op jit(solution)/shard_map/all_to_all | solution.py:161
  276.8 1.5 dynamic-slice_bitcast_fusion.3
  278.3 0.7 dynamic-slice_bitcast_fusion
  279.0 0.7 dynamic-slice_bitcast_fusion.1
  279.6 0.7 dynamic-slice_bitcast_fusion.2
  280.3 5.4 %all-to-all-done.1 = bf16[4,128,512]{2,1,0:T(8,128)(2,1)} async-done(((bf16[4,128,512]{2,1,0:T(8,128)(2,1)}), bf16[4,128,512]{2,1,0:T(8,128)(2,1)}, u32[]{:S(2)}, u32[]{:S(2)}) %all-to-all-start.1) | async-done | bytes 524320 | tf_op jit(solution)/shard_map/all_to_all | solution.py:161
  285.7 1.6 fusion.11
  287.3 0.3 copy.47
  287.6 1.0 copy.48
  (44 shorter events, 0.2 us)
Async XLA Ops:
  7.2 4.4 %copy-start.17 = (bf16[1,64,512]{2,1,0:T(8,128)(2,1)S(1)}, bf16[1,64,512]{2,1,0:T(8,128)(2,1)}, u32[]{:S(2)}) copy-start(bf16[1,64,512]{2,1,0:T(8,128)(2,1)} %param.16) | copy-start | bytes 196612
  7.2 37.5 %copy-start.18 = (bf16[1,64,512]{2,1,0:T(8,128)(2,1)S(1)}, bf16[1,64,512]{2,1,0:T(8,128)(2,1)}, u32[]{:S(2)}) copy-start(bf16[1,64,512]{2,1,0:T(8,128)(2,1)} %param.17) | copy-start | bytes 196612
  7.2 69.0 %copy-start.19 = (bf16[1,64,512]{2,1,0:T(8,128)(2,1)S(1)}, bf16[1,64,512]{2,1,0:T(8,128)(2,1)}, u32[]{:S(2)}) copy-start(bf16[1,64,512]{2,1,0:T(8,128)(2,1)} %param.18) | copy-start | bytes 196612
  7.2 100.1 %all-gather.6.cloned.1.call-start = ((), (), s32[]{:S(2)}) async-start(), calls=%async_computation.2 | async-start | bytes 2621440 | tf_op jit(solution)/shard_map/all_gather | solution.py:139
  9.3 103.0 %all-gather.8.cloned.1.call-start = ((), (), s32[]{:S(2)}) async-start(), calls=%async_computation.3 | async-start | bytes 2621440 | tf_op jit(solution)/shard_map/all_gather | solution.py:140
  11.5 241.8 %all-reduce.3.cloned.1.call-start = ((), (), s32[]{:S(2)}) async-start(), calls=%async_computation.4 | async-start | bytes 6291456 | tf_op jit(solution)/shard_map/psum | solution.py:109
  44.7 67.6 %copy-start.3 = (bf16[1,512,512]{2,1,0:T(8,128)(2,1)}, bf16[1,512,512]{2,1,0:T(8,128)(2,1)S(1)}, u32[]{:S(2)}) copy-start(bf16[1,512,512]{2,1,0:T(8,128)(2,1)S(1)} %all-gather) | copy-start | bytes 1572868
  76.1 36.2 %copy-start.5 = (bf16[1,512,512]{2,1,0:T(8,128)(2,1)}, bf16[1,512,512]{2,1,0:T(8,128)(2,1)S(1)}, u32[]{:S(2)}) copy-start(bf16[1,512,512]{2,1,0:T(8,128)(2,1)S(1)} %all-gather.2) | copy-start | bytes 1572868
  112.3 1.8 copy-start.7
  114.1 2.4 copy-start.14
  114.1 2.4 copy-start.10
  114.1 2.4 copy-start.11
  116.5 2.9 copy-start.9
  119.4 1.6 copy-start.15
  119.4 1.6 copy-start.16
  121.1 1.8 copy-start.13
  122.9 4.5 %copy-start.21 = (s32[1,4]{1,0:T(1,128)S(1)}, s32[1,4]{1,0:T(1,128)}, u32[]{:S(2)}) copy-start(s32[1,4]{1,0:T(1,128)} %param.14) | copy-start | bytes 52
  122.9 4.7 %copy-start.20 = (f32[2048]{0:T(1024)S(1)}, f32[2048]{0:T(1024)}, u32[]{:S(2)}) copy-start(f32[2048]{0:T(1024)} %param.15) | copy-start | bytes 24580
  123.9 12.3 %all-to-all-start = ((bf16[128,4,512]{0,2,1:T(8,128)(2,1)}), bf16[128,4,512]{0,2,1:T(8,128)(2,1)S(1)}, u32[]{:S(2)}, u32[]{:S(2)}) async-start(bf16[128,4,512]{0,2,1:T(8,128)(2,1)} %bitcast.2), calls=%async_computation | async-start | bytes 1048576 | tf_op jit(solution)/shard_map/all_to_all | solution.py:155
  253.2 5.7 %copy-start.2 = (f32[512,512]{1,0:T(8,128)S(1)}, f32[512,512]{1,0:T(8,128)}, u32[]{:S(2)}) copy-start(f32[512,512]{1,0:T(8,128)} %get-tuple-element.82) | copy-start | bytes 3145732
  259.8 2.2 copy-start.1
  260.9 2.5 copy-start.6
  261.9 1.7 copy-start
  262.0 1.8 copy-start.4
  263.7 1.2 copy-start.12
  263.7 1.9 copy-start.8
  272.7 13.0 %all-to-all-start.1 = ((bf16[4,128,512]{2,1,0:T(8,128)(2,1)}), bf16[4,128,512]{2,1,0:T(8,128)(2,1)}, u32[]{:S(2)}, u32[]{:S(2)}) async-start(bf16[4,128,512]{2,1,0:T(8,128)(2,1)} %bitcast.90), calls=%async_computation.1 | async-start | bytes 1048576 | tf_op jit(solution)/shard_map/all_to_all | solution.py:161
Sparse Core Ops, SparseCore 0:
  10.1 25.5 all-gather.5
  37.3 22.8 all-gather.7
  123.0 130.1 all-reduce.2
where the time goes:
time: 296 us; the launch traced here: 295 us
  waiting for transfers between devices  121 us (41%)
  blocking collectives  95.8 us (32%)
  matrix products  25.4 us (9%)
  other arithmetic  16.7 us (6%)
  between operations  16.2 us (5%)
  local copies, waits for them, and re-layouts  12.5 us (4%)
  starting transfers between devices  7.72 us (3%)
    psum x1, waiting for transfers between devices, fast_branch(): full_moments = lax.psum(placed, 'wide')  107 us
    all_gather x1, blocking collectives, fast_branch(): lax.all_gather(weights[0], 'wide', axis=0, tiled=True)  33.2 us
    all_gather x1, blocking collectives, fast_branch(): lax.all_gather(weights[1], 'wide', axis=0, tiled=True)  31.4 us
    all_gather x1, blocking collectives, fast_branch(): lax.all_gather(weights[2], 'wide', axis=0, tiled=True)  31.2 us
    all_to_all x1, waiting for transfers between devices, per_device(): lax.all_to_all(queries, 'narrow', split_axis=1, concat_axis=0, tiled=True)  8.22 us
    unnamed x48, local copies, waits for them, and re-layouts  6.28 us
  transfers between devices with their start and end apart: 5, of which 3 were waited for; matrix products, arithmetic and copies ran while one was open for 7% of the time, Pallas kernels for 0%

commit v1 on v0

--- a/solution.py
+++ b/solution.py
@@ -1,11 +1,379 @@
 import jax
 import jax.numpy as jnp
 from jax import lax
+from jax.experimental import pallas as pl
+from jax.experimental.pallas import tpu as pltpu
 from jax.sharding import PartitionSpec as P
+
 
 momentum_decay = 0.9
 step_size = 0.02
 epsilon = 1e-06
+bf16 = jnp.bfloat16
+f32 = jnp.float32
+
+
+VMEM = pl.BlockSpec(memory_space=pltpu.VMEM)
+SMEM = pl.BlockSpec(memory_space=pltpu.SMEM)
+ANY = pl.BlockSpec(memory_space=pltpu.HBM)
+PAD = 16
+
+
+def shape_of(shape, dtype):
+    return jax.ShapeDtypeStruct(shape, dtype)
+
+
+def call(kernel, out_shape, operands, scratch=(), mib=16, smem=(), far=()):
+    return pl.pallas_call(
+        kernel,
+        out_shape=out_shape,
+        in_specs=[
+            SMEM if i in smem else ANY if i in far else VMEM for i in range(len(operands))
+        ],
+        out_specs=[VMEM] * len(out_shape),
+        scratch_shapes=list(scratch),
+        compiler_params=pltpu.CompilerParams(vmem_limit_bytes=mib * 2**20),
+    )(*operands)
+
+
+def mm(a, b):
+    return jnp.dot(a, b, preferred_element_type=f32)
+
+
+def mm_nt(a, b):
+    return lax.dot_general(a, b, (((1,), (1,)), ((), ())), preferred_element_type=f32)
+
+
+def mm_tn(a, b):
+    return lax.dot_general(a, b, (((0,), (0,)), ((), ())), preferred_element_type=f32)
+
+
+class Plan:
+    def __init__(self, mesh, rows, tokens, head_size, views):
+        self.wide = mesh.shape["wide"]
+        self.narrow = mesh.shape["narrow"]
+        self.rest = self.wide // 2
+        self.rows, self.tokens, self.head_size, self.views = rows, tokens, head_size, views
+
+    def place(self, group, head):
+        return (group // 2 * 2 + head % 2, head // 2 * 2 + group % 2)
+
+    def home(self, group, head):
+        return (group, head)
+
+    def role(self):
+        w, n = lax.axis_index("wide"), lax.axis_index("narrow")
+        return w // 2 * 2 + n % 2, n // 2 * 2 + w % 2
+
+    def send(self, x, source, target):
+        pairs = []
+        for a in range(self.wide):
+            for b in range(self.narrow):
+                s, t = source(a, b), target(a, b)
+                pairs.append((s[0] * self.narrow + s[1], t[0] * self.narrow + t[1]))
+        return lax.ppermute(x, ("wide", "narrow"), pairs)
+
+    def partner(self, x):
+        return self.send(x, self.place, lambda a, b: self.place(a ^ 1, b))
+
+    def along(self, x, k):
+        return self.send(x, self.place, lambda a, b: self.place((a + 2 * k) % self.wide, b))
+
+    def to_head(self, x, k):
+        return self.send(x, self.home, lambda a, b: self.place(a, (b + k) % self.narrow))
+
+    def to_tokens(self, x, k):
+        return self.send(x, self.place, lambda a, b: (a, (b - k) % self.narrow))
+
+    def starts(self, k, other):
+        group, _ = self.role()
+        z, c = group // 2, group % 2
+        r = lax.rem(z + self.rest - k, self.rest)
+        return pl.multiple_of((2 * r + (1 - c if other else c)) * self.rows, self.rows)
+
+    def goes(self, k, other):
+        group, _ = self.role()
+        z, c = group // 2, group % 2
+        r = lax.rem(z + k, self.rest)
+        return pl.multiple_of((2 * r + (1 - c if other else c)) * self.rows, self.rows)
+
+
+def columns_at(plan, ref, k):
+    head = lax.rem(lax.axis_index("narrow") + k, plan.narrow)
+    size = plan.head_size
+    return ref.at[:, pl.ds(pl.multiple_of(head * size, size), size)]
+
+
+def stacked(parts):
+    total, top, out = sum(x.shape[0] for x in parts), 0, None
+    for x in parts:
+        bottom = total - top - x.shape[0]
+        padded = lax.pad(x, jnp.zeros((), x.dtype), ((top, bottom, 0), (0, 0, 0)))
+        out = padded if out is None else out + padded
+        top += x.shape[0]
+    return out
+
+
+def head_columns(plan, x, k):
+    head = lax.rem(lax.axis_index("narrow") + k, plan.narrow)
+    return lax.dynamic_slice_in_dim(x, head * plan.head_size, plan.head_size, 1)
+
+
+def pack_queries(plan, lengths, queries, moments):
+    rows, tb, hs = plan.rows, plan.tokens, plan.head_size
+
+    def kernel(len_ref, q_ref, *refs):
+        ms, first, others = refs[:3], refs[3], refs[4:]
+        first[:tb, :] = columns_at(plan, q_ref, 0)[...]
+        for i in range(3):
+            first[tb + i * rows : tb + (i + 1) * rows, :] = ms[i][0].astype(bf16)
+        line = lax.broadcasted_iota(jnp.int32, (PAD, hs), 0)
+        table = jnp.zeros((PAD, hs), jnp.int32)
+        for i in range(plan.views):
+            table = jnp.where(line == i, len_ref[0, i], table)
+        first[tb + 3 * rows :, :] = table.astype(f32).astype(bf16)
+        for k, out in enumerate(others):
+            out[...] = columns_at(plan, q_ref, k + 1)[...]
+
+    shapes = [shape_of((tb + 3 * rows + PAD, hs), bf16)]
+    shapes += [shape_of((tb, hs), bf16)] * (plan.narrow - 1)
+    return call(kernel, shapes, [lengths, queries, *moments], mib=8, smem=(0,))
+
+
+def grads_call(plan, kv, w_own, w_other):
+    rows, tb, hs = plan.rows, plan.tokens, plan.head_size
+    blocks, rest = plan.narrow, plan.rest
+    total = blocks * tb
+
+    def kernel(*refs):
+        kv = refs[:blocks]
+        w_own = refs[blocks : blocks + rest - 1]
+        w_other = refs[blocks + rest - 1 : blocks + 2 * rest - 1]
+        w_full, part, own, tmp, k_all, v_all, hid, dg, du = refs[blocks + 2 * rest - 1 :]
+        for other, chunks in enumerate(((kv[0], *w_own), w_other)):
+            for k, chunk in enumerate(chunks):
+                at = plan.starts(k, other)
+                for i in range(3):
+                    if k == 0:
+                        first = 2 * tb + i * rows
+                        piece = chunk[first : first + rows, :]
+                    else:
+                        piece = chunk[i]
+                    w_full[i, pl.ds(at, rows), :] = piece
+        for b in range(blocks):
+            at = slice(b * tb, (b + 1) * tb)
+            k, v = kv[b][:tb, :], kv[b][tb : 2 * tb, :]
+            k_all[at, :] = k
+            v_all[at, :] = v
+            pre_gate = mm(k, w_full[0])
+            pre_up = mm(k, w_full[1])
+            d_hidden = -mm_nt(v, w_full[2])
+            sig = 1.0 / (1.0 + jnp.exp(-pre_gate))
+            activ = pre_gate * sig
+            hid[at, :] = (activ * pre_up).astype(bf16)
+            slope = sig * (1.0 + pre_gate * (1.0 - sig))
+            dg[at, :] = (d_hidden * pre_up * slope).astype(bf16)
+            du[at, :] = (d_hidden * activ).astype(bf16)
+        for i, (left, right) in enumerate(((k_all, dg), (k_all, du), (hid, v_all))):
+            grad = mm_tn(left[...], right[...])
+            tmp[i] = -grad if i == 2 else grad
+            for k in range(rest):
+                own[k, i] = tmp[i, pl.ds(plan.goes(k, 0), rows), :]
+                part[k, i] = tmp[i, pl.ds(plan.goes(k, 1), rows), :].astype(bf16)
+
+    shapes = [
+        shape_of((3, hs, hs), bf16),
+        shape_of((rest, 3, rows, hs), bf16),
+        shape_of((rest, 3, rows, hs), f32),
+    ]
+    scratch = [pltpu.VMEM((3, hs, hs), f32)]
+    scratch += [pltpu.VMEM((total, hs), bf16) for _ in range(5)]
+    return call(kernel, shapes, [*kv, *w_own, *w_other], scratch, mib=20)
+
+
+def share_call(plan, own, part):
+    rows, hs, rest = plan.rows, plan.head_size, plan.rest
+
+    def kernel(own_ref, part_ref, kept, *outs):
+        kept[...] = own_ref[0] + part_ref[0].astype(f32)
+        for k, out in enumerate(outs):
+            out[...] = (own_ref[k + 1] + part_ref[k + 1].astype(f32)).astype(bf16)
+
+    shapes = [shape_of((3, rows, hs), f32)] + [shape_of((3, rows, hs), bf16)] * (rest - 1)
+    return call(kernel, shapes, [own, part], mib=4)
+
+
+def moment_call(plan, kept, arrived, first_q, scale):
+    rows, tb, hs = plan.rows, plan.tokens, plan.head_size
+
+    def kernel(kept_ref, q_ref, *refs):
+        arrived, got, mom = refs[:-2], refs[-2], refs[-1]
+        for i in range(3):
+            grad = kept_ref[i]
+            for x in arrived:
+                grad = grad + x[i].astype(f32)
+            grad = grad * scale
+            got[i] = grad
+            old = q_ref[tb + i * rows : tb + (i + 1) * rows, :].astype(f32)
+            mom[i] = (momentum_decay * old + grad).astype(bf16)
+
+    shapes = [shape_of((3, rows, hs), f32), shape_of((3, rows, hs), bf16)]
+    return call(kernel, shapes, [kept, first_q, *arrived], mib=4)
+
+
+def attend_call(plan, q, kv, gains):
+    rows, tb, hs = plan.rows, plan.tokens, plan.head_size
+    blocks = plan.narrow
+
+    def kernel(gain_ref, *refs):
+        q, kv, out = refs[:blocks], refs[blocks : 2 * blocks], refs[2 * blocks]
+        k_all, v_all = refs[2 * blocks + 1 :]
+        _, head = plan.role()
+        gain = gain_ref[:, pl.ds(pl.multiple_of(head * hs, hs), hs)]
+        table = q[0][tb + 3 * rows :, :].astype(f32)
+        ends, end = [], 0.0
+        for i in range(plan.views - 1):
+            end = end + table[i : i + 1, :1]
+            ends.append(end)
+
+        def view_of(pos):
+            number = jnp.zeros(pos.shape, f32)
+            for e in ends:
+                number = number + (pos.astype(f32) >= e).astype(f32)
+            return number
+
+        key_views = []
+        for b in range(blocks):
+            at = slice(b * tb, (b + 1) * tb)
+            k_all[at, :] = kv[b][:tb, :]
+            v_all[at, :] = kv[b][tb : 2 * tb, :]
+            quarter = lax.rem(head + blocks - b, blocks)
+            key_views.append(
+                view_of(quarter * tb + lax.broadcasted_iota(jnp.int32, (1, tb), 1))
+            )
+        key_views = jnp.concatenate(key_views, axis=1)
+        for b in range(blocks):
+            quarter = lax.rem(head + blocks - b, blocks)
+            row_views = view_of(quarter * tb + lax.broadcasted_iota(jnp.int32, (tb, 1), 0))
+            scores = mm_nt(q[b][:tb, :], k_all[...]) * (hs ** (-0.5))
+            scores = jnp.where(row_views == key_views, scores, -1e30)
+            expo = jnp.exp(scores - jnp.max(scores, axis=-1, keepdims=True))
+            probs = (expo / jnp.sum(expo, axis=-1, keepdims=True)).astype(bf16)
+            attn = mm(probs, v_all[...])
+            norm = lax.rsqrt(jnp.mean(attn * attn, axis=-1, keepdims=True) + epsilon)
+            out[b] = (attn * norm * gain).astype(bf16)
+
+    shapes = [shape_of((blocks, tb, hs), bf16)]
+    scratch = [pltpu.VMEM((blocks * tb, hs), bf16) for _ in range(2)]
+    return call(kernel, shapes, [gains, *q, *kv], scratch, mib=14)[0]
+
+
+def fast_call(plan, q, view_out, w_full, m_own, m_other, gains):
+    rows, tb, hs = plan.rows, plan.tokens, plan.head_size
+    blocks, rest = plan.narrow, plan.rest
+
+    def kernel(gain_ref, view_ref, w_ref, *refs):
+        q = refs[:blocks]
+        chunks = refs[blocks : blocks + 2 * rest]
+        outs = refs[blocks + 2 * rest : 2 * blocks + 2 * rest]
+        mom, new = refs[2 * blocks + 2 * rest :]
+        group, head = plan.role()
+        gain = gain_ref[:, pl.ds(pl.multiple_of(head * hs, hs), hs)]
+        for j, chunk in enumerate(chunks):
+            at = plan.starts(j % rest, j // rest)
+            for i in range(3):
+                mom[i, pl.ds(at, rows), :] = chunk[i]
+        part = min(128, hs)
+        for i in range(3):
+            squares = jnp.zeros((part, hs), f32)
+            for s in range(0, hs, part):
+                piece = mom[i, s : s + part, :].astype(f32)
+                squares = squares + piece * piece
+            radius = jnp.sqrt(jnp.sum(squares) / float(hs * hs) + epsilon)
+            for s in range(0, hs, part):
+                old = w_ref[i, s : s + part, :].astype(f32)
+                moved = old - step_size * mom[i, s : s + part, :].astype(f32) / radius
+                ratio = jnp.sqrt(
+                    jnp.sum(old * old, axis=-1, keepdims=True) + epsilon
+                ) / jnp.sqrt(jnp.sum(moved * moved, axis=-1, keepdims=True) + epsilon)
+                new[i, s : s + part, :] = (moved * ratio).astype(bf16)
+        start = pl.multiple_of(group * rows, rows)
+        for i in range(3):
+            outs[0][tb + i * rows : tb + (i + 1) * rows, :] = new[i, pl.ds(start, rows), :]
+        for b in range(blocks):
+            rows_q = q[b][:tb, :]
+            pre_gate = mm(rows_q, new[0])
+            pre_up = mm(rows_q, new[1])
+            hidden = (pre_gate / (1.0 + jnp.exp(-pre_gate)) * pre_up).astype(bf16)
+            raw = mm(hidden, new[2])
+            norm = lax.rsqrt(jnp.mean(raw * raw, axis=-1, keepdims=True) + epsilon)
+            fast = (raw * norm * gain).astype(bf16)
+            outs[b][:tb, :] = (view_ref[b].astype(f32) + fast.astype(f32)).astype(bf16)
+
+    shapes = [shape_of((tb + 3 * rows, hs), bf16)]
+    shapes += [shape_of((tb, hs), bf16)] * (blocks - 1)
+    scratch = [pltpu.VMEM((3, hs, hs), bf16) for _ in range(2)]
+    operands = [gains, view_out, w_full, *q, *m_own, *m_other]
+    return call(kernel, shapes, operands, scratch, mib=18)
+
+
+def finish_call(plan, blocks):
+    rows, tb, hs = plan.rows, plan.tokens, plan.head_size
+    count = plan.narrow
+
+    def kernel(*refs):
+        out, fresh = refs[count], refs[count + 1 :]
+        n = lax.axis_index("narrow")
+        for b in range(count):
+            head = lax.rem(n + b, count)
+            out[:, pl.ds(pl.multiple_of(head * hs, hs), hs)] = refs[b][:tb, :]
+        for i in range(3):
+            fresh[i][0] = refs[0][tb + i * rows : tb + (i + 1) * rows, :]
+
+    shapes = [shape_of((tb, hs * count), bf16)] + [shape_of((1, rows, hs), bf16)] * 3
+    return call(kernel, shapes, blocks, mib=6)
+
+
+def per_device(
+    plan, queries, keys, values, view_lengths, gain, w_gate, w_up, w_down, m_gate, m_up, m_down
+):
+    narrow, rest = plan.narrow, plan.rest
+    scale = float(plan.tokens * narrow * plan.wide) ** (-0.5)
+    gains = gain.reshape(1, narrow * plan.head_size)
+    moments = (m_gate, m_up, m_down)
+
+    weights = [w_gate, w_up, w_down]
+    flat_w = [x[0] for x in weights]
+    packed_w = stacked(flat_w).reshape(3, plan.rows, plan.head_size)
+    w_own = [
+        plan.send(packed_w, plan.home, lambda a, b: plan.place((a + 2 * k) % plan.wide, b))
+        for k in range(1, rest)
+    ]
+    pairs = []
+    for k in range(narrow):
+        parts = [head_columns(plan, keys, k), head_columns(plan, values, k)]
+        pairs.append(stacked(parts + flat_w if k == 0 else parts))
+    kv = [plan.to_head(x, k) for k, x in enumerate(pairs)]
+    w_other = [plan.partner(x) for x in (kv[0], *w_own)]
+    w_full, part, own = grads_call(plan, kv, w_own, w_other)
+
+    kept, *shares = share_call(plan, own, plan.partner(part))
+    packed_q = pack_queries(plan, view_lengths, queries, moments)
+    arrived = [plan.along(x, k + 1) for k, x in enumerate(shares)]
+    q = [plan.to_head(x, k) for k, x in enumerate(packed_q)]
+    view_out = attend_call(plan, q, kv, gains)
+
+    got, mom = moment_call(plan, kept, arrived, q[0], scale)
+    m_own = [mom] + [plan.along(mom, k) for k in range(1, rest)]
+    m_other = [plan.partner(x) for x in m_own]
+    got = plan.send(got, plan.place, plan.home)
+    new_moments = [
+        momentum_decay * moment + got[i][None] for i, moment in enumerate(moments)
+    ]
+    outs = fast_call(plan, q, view_out, w_full, m_own, m_other, gains)
+    outs = [plan.to_tokens(x, k) for k, x in enumerate(outs)]
+    output, *fresh = finish_call(plan, outs)
+    return (output, *fresh, *new_moments)
 
 
 def attend(query_rows, key_rows, value_rows, query_ids, key_ids):
@@ -53,7 +421,6 @@
     block = min(row_total, 512)
 
     def add_block(number, totals):
-        start = number * block
         terms = block_gradients(key_rows, value_rows, gate_full, up_full, down_full)
         return tuple((total + term for total, term in zip(totals, terms)))
 
@@ -121,7 +488,7 @@
     return (fast_out, fresh, moment_new)
 
 
-def per_device(
+def per_device_general(
     queries, keys, values, view_lengths, gain, w_gate, w_up, w_down, m_gate, m_up, m_down
 ):
     narrow_size = lax.axis_size("narrow")
@@ -172,28 +539,22 @@
 
 
 def solution(mesh):
-    in_specs = (
-        P(("wide", "narrow"), None),
-        P(("wide", "narrow"), None),
-        P(("wide", "narrow"), None),
-        P("wide", None),
-        P(),
-        P("narrow", "wide", None),
-        P("narrow", "wide", None),
-        P("narrow", "wide", None),
-        P("narrow", "wide", None),
-        P("narrow", "wide", None),
-        P("narrow", "wide", None),
-    )
-    out_specs = (
-        P(("wide", "narrow"), None),
-        P("narrow", "wide", None),
-        P("narrow", "wide", None),
-        P("narrow", "wide", None),
-        P("narrow", "wide", None),
-        P("narrow", "wide", None),
-        P("narrow", "wide", None),
-    )
+    wide, narrow = mesh.shape["wide"], mesh.shape["narrow"]
+    paired = wide % 2 == 0 and narrow % 2 == 0 and wide <= 16
+
+    def body(queries, keys, values, view_lengths, *args):
+        operands = (queries, keys, values, view_lengths, *args)
+        if not paired:
+            return per_device_general(*operands)
+        tokens, width = queries.shape
+        rows, views = args[1].shape[1], view_lengths.shape[1]
+        plan = Plan(mesh, rows, tokens, width // narrow, views)
+        return per_device(plan, *operands)
+
+    tokens = P(("wide", "narrow"), None)
+    state = P("narrow", "wide", None)
+    in_specs = (tokens, tokens, tokens, P("wide", None), P()) + (state,) * 6
+    out_specs = (tokens,) + (state,) * 6
     return jax.shard_map(
-        per_device, mesh=mesh, in_specs=in_specs, out_specs=out_specs, check_vma=False
-    )
+        body, mesh=mesh, in_specs=in_specs, out_specs=out_specs, check_vma=False
+    )

time: 296 us -> 94.3 us (0.32)
  the two profiles are of different devices: /device:TPU:0 before, /device:TPU:24 now
where the time goes in v1:
time: 94.3 us; the launch traced here: 94.1 us
  starting transfers between devices  43.9 us (47%)
  waiting for transfers between devices  36.4 us (39%)
  Pallas kernels  10.6 us (11%)
  local copies, waits for them, and re-layouts  1.47 us (2%)
  between operations  0.99 us (1%)
    ppermute x31, starting transfers between devices, send(): return lax.ppermute(x, ('wide', 'narrow'), pairs)  43.9 us
    ppermute x31, waiting for transfers between devices, send(): return lax.ppermute(x, ('wide', 'narrow'), pairs)  36.4 us
    pallas_call x7, Pallas kernels, call(): pl.pallas_call(kernel, out_shape=out_shape, in_specs=[SMEM if i in smem e...  10.6 us
  transfers between devices with their start and end apart: 31, of which 8 were waited for; matrix products, arithmetic and copies ran while one was open for 1% of the time, Pallas kernels for 8%

profile of v1, /device:TPU:24, one launch (start us, length us, event | category | flops | bytes accessed | tf_op | source)
XLA Modules:
  0.0 94.1 jit_solution(26536603686916089)
XLA Ops:
  0.7 1.4 %constant_dynamic-slice_fusion = (bf16[128,512]{1,0:T(8,128)(2,1)S(1)}, bf16[128,512]{1,0:T(8,128)(2,1)S(1)}, bf16[128,512]{1,0:T(8,128)(2,1)S(1)}, bf16[128,512...) fusion(bf16[128,2048]{1,0:T(8,128)(2,1)} %param.13, ...), kind=kLoop, calls=%fused_computation.8 | loop fusion | bytes 2097168 | tf_op jit(solution)/shard_map/dynamic_slice | solution.py:119
  2.2 0.7 collective-permute-start.4
  2.9 0.1 collective-permute-start.8
  3.0 1.9 %collective-permute-start.9 = (bf16[3,64,512]{2,1,0:T(8,128)(2,1)S(1)}, bf16[3,64,512]{2,1,0:T(8,128)(2,1)S(1)}, u32[]{:S(2)}, u32[]{:S(2)}) collective-permute-start(bf16[3,64,512]{2,1,0:T(8,128)(2,1)S(1)} %bitcast.14), channel_id=1, source_target_pairs={{0,16},{1,20},{2,18},{3,22},{4,17},{5,21},{6,19},{7,23},{8,24},{9,... | collective-permute-start | bytes 589832 | tf_op jit(solution)/shard_map/ppermute | solution.py:74
  4.9 3.4 %collective-permute-start.5 = (bf16[256,512]{1,0:T(8,128)(2,1)S(1)}, bf16[256,512]{1,0:T(8,128)(2,1)S(1)}, u32[]{:S(2)}, u32[]{:S(2)}) collective-permute-start(bf16[256,512]{1,0:T(8,128)(2,1)S(1)} %pad_add_fusion.3), channel_id=1, source_target_pairs={{0,4},{1,2},{2,6},{3,0},{4,5},{5,3},{6,7},{7,1},{8,12},{9,10},{10,... | collective-permute-start | bytes 786440 | tf_op jit(solution)/shard_map/ppermute | solution.py:74
  8.3 1.6 %collective-permute-start.6 = (bf16[256,512]{1,0:T(8,128)(2,1)S(1)}, bf16[256,512]{1,0:T(8,128)(2,1)S(1)}, u32[]{:S(2)}, u32[]{:S(2)}) collective-permute-start(bf16[256,512]{1,0:T(8,128)(2,1)S(1)} %pad_add_fusion.2), channel_id=1, source_target_pairs={{0,2},{1,6},{2,0},{3,4},{4,3},{5,7},{6,1},{7,5},{8,10},{9,14},{10,... | collective-permute-start | bytes 786440 | tf_op jit(solution)/shard_map/ppermute | solution.py:74
  9.9 0.0 collective-permute-done.4.refs_4_.refs_0_
  9.9 6.4 %collective-permute-start.11 = (bf16[448,512]{1,0:T(8,128)(2,1)S(1)}, bf16[448,512]{1,0:T(8,128)(2,1)S(1)}, u32[]{:S(2)}, u32[]{:S(2)}) collective-permute-start(bf16[448,512]{1,0:T(8,128)(2,1)S(1)} %collective-permute-done.4.refs_4_.refs_0_), channel_id=1, source_target_pairs={{0,1},{4,5},{2,3},{6,7},{1,0},{5,4},{3,2},{7,6},{8,9},{12,13},{10,... | collective-permute-start | bytes 1376264 | tf_op jit(solution)/shard_map/ppermute | solution.py:74
  16.4 1.7 %collective-permute-start.10 = (bf16[3,64,512]{2,1,0:T(8,128)(2,1)S(1)}, bf16[3,64,512]{2,1,0:T(8,128)(2,1)S(1)}, u32[]{:S(2)}, u32[]{:S(2)}) collective-permute-start(bf16[3,64,512]{2,1,0:T(8,128)(2,1)S(1)} %bitcast.15), channel_id=1, source_target_pairs={{0,24},{1,28},{2,26},{3,30},{4,25},{5,29},{6,27},{7,31},{8,0},{9,4... | collective-permute-start | bytes 589832 | tf_op jit(solution)/shard_map/ppermute | solution.py:74
  18.1 0.0 copy-start
  18.1 0.0 copy-start.1
  18.1 0.0 copy-start.2
  18.1 0.0 copy-start.3
  18.1 0.0 copy-start.5
  18.1 0.0 collective-permute-done.9.refs_5_
  18.1 3.5 %collective-permute-start.7 = (bf16[256,512]{1,0:T(8,128)(2,1)S(1)}, bf16[256,512]{1,0:T(8,128)(2,1)S(1)}, u32[]{:S(2)}, u32[]{:S(2)}) collective-permute-start(bf16[256,512]{1,0:T(8,128)(2,1)S(1)} %pad_add_fusion.1), channel_id=1, source_target_pairs={{0,6},{1,0},{2,4},{3,2},{4,7},{5,1},{6,5},{7,3},{8,14},{9,8},{10,1... | collective-permute-start | bytes 786440 | tf_op jit(solution)/shard_map/ppermute | solution.py:74
  21.6 2.9 %collective-permute-done.10.refs_6_ = bf16[3,64,512]{2,1,0:T(8,128)(2,1)S(1)} collective-permute-done((bf16[3,64,512]{2,1,0:T(8,128)(2,1)S(1)}, bf16[3,64,512]{2,1,0:T(8,128)(2,1)S(1)}, u32[]{:S(2)}, u32[]{:S(2)}) %collective-permute-start.10) | collective-permute-done | bytes 196640 | tf_op jit(solution)/shard_map/ppermute | solution.py:74
  24.5 0.7 collective-permute-start.12
  25.3 0.0 collective-permute-start.13
  25.3 0.0 collective-permute-done.6.refs_6_.refs_2_
  25.3 0.5 collective-permute-start.14
  25.8 1.5 %collective-permute-done.7.refs_7_.refs_3_ = bf16[256,512]{1,0:T(8,128)(2,1)S(1)} collective-permute-done((bf16[256,512]{1,0:T(8,128)(2,1)S(1)}, bf16[256,512]{1,0:T(8,128)(2,1)S(1)}, u32[]{:S(2)}, u32[]{:S(2)}) %collective-permute-start.7) | collective-permute-done | bytes 262176 | tf_op jit(solution)/shard_map/ppermute | solution.py:74
  27.3 0.0 collective-permute-done.12.refs_8_
  27.3 0.0 collective-permute-done.11.refs_7_
  27.3 2.6 %shard_map.164 = (bf16[3,512,512]{2,1,0:T(8,128)(2,1)S(1)}, bf16[4,3,64,512]{3,2,1,0:T(8,128)(2,1)S(1)}, f32[4,3,64,512]{3,2,1,0:T(8,128)S(1)}) custom-call(bf16[448,512]{1,0:T(8,128)(2,1)S(1)} %collective-permute-done.4.refs_4_.refs_0_, bf16[256,512]{1,0:T(8,128)(2,1)S(1)} %collective-permute-done.5.refs_5_.refs_1_, ...), custom_call_target="tpu_custom_call" | custom-call | tf_op jit(solution)/shard_map/pallas_call | solution.py:27
  29.9 0.1 collective-permute-start.15
  30.1 0.6 shard_map.162
  30.7 0.7 collective-permute-start
  31.4 0.9 collective-permute-done.15.part_ref
  32.3 0.2 shard_map.165
  32.5 1.0 %collective-permute-start.16 = (bf16[3,64,512]{2,1,0:T(8,128)(2,1)S(1)}, bf16[3,64,512]{2,1,0:T(8,128)(2,1)S(1)}, u32[]{:S(2)}, u32[]{:S(2)}) collective-permute-start(bf16[3,64,512]{2,1,0:T(8,128)(2,1)S(1)} %get-tuple-element.36), channel_id=1, source_target_pairs={{0,8},{4,12},{2,10},{6,14},{1,9},{5,13},{3,11},{7,15},{8,16},{12,2... | collective-permute-start | bytes 589832 | tf_op jit(solution)/shard_map/ppermute | solution.py:74
  33.5 0.4 collective-permute-start.17
  33.9 1.9 %collective-permute-start.18 = (bf16[3,64,512]{2,1,0:T(8,128)(2,1)S(1)}, bf16[3,64,512]{2,1,0:T(8,128)(2,1)S(1)}, u32[]{:S(2)}, u32[]{:S(2)}) collective-permute-start(bf16[3,64,512]{2,1,0:T(8,128)(2,1)S(1)} %get-tuple-element.38), channel_id=1, source_target_pairs={{0,24},{4,28},{2,26},{6,30},{1,25},{5,29},{3,27},{7,31},{8,0},{12,... | collective-permute-start | bytes 589832 | tf_op jit(solution)/shard_map/ppermute | solution.py:74
  35.8 2.4 %collective-permute-start.1 = (bf16[128,512]{1,0:T(8,128)(2,1)S(1)}, bf16[128,512]{1,0:T(8,128)(2,1)S(1)}, u32[]{:S(2)}, u32[]{:S(2)}) collective-permute-start(bf16[128,512]{1,0:T(8,128)(2,1)S(1)} %get-tuple-element.29), channel_id=1, source_target_pairs={{0,4},{1,2},{2,6},{3,0},{4,5},{5,3},{6,7},{7,1},{8,12},{9,10},{10,... | collective-permute-start | bytes 393224 | tf_op jit(solution)/shard_map/ppermute | solution.py:74
  38.2 0.0 collective-permute-done.refs_0_.q_ref
  38.2 1.5 %collective-permute-start.2 = (bf16[128,512]{1,0:T(8,128)(2,1)S(1)}, bf16[128,512]{1,0:T(8,128)(2,1)S(1)}, u32[]{:S(2)}, u32[]{:S(2)}) collective-permute-start(bf16[128,512]{1,0:T(8,128)(2,1)S(1)} %get-tuple-element.30), channel_id=1, source_target_pairs={{0,2},{1,6},{2,0},{3,4},{4,3},{5,7},{6,1},{7,5},{8,10},{9,14},{10,... | collective-permute-start | bytes 393224 | tf_op jit(solution)/shard_map/ppermute | solution.py:74
  39.7 0.0 collective-permute-done.16.refs_0_
  39.7 10.8 %collective-permute-done.17.refs_1_ = bf16[3,64,512]{2,1,0:T(8,128)(2,1)S(1)} collective-permute-done((bf16[3,64,512]{2,1,0:T(8,128)(2,1)S(1)}, bf16[3,64,512]{2,1,0:T(8,128)(2,1)S(1)}, u32[]{:S(2)}, u32[]{:S(2)}) %collective-permute-start.17) | collective-permute-done | bytes 196640 | tf_op jit(solution)/shard_map/ppermute | solution.py:74
  50.6 0.1 shard_map.166
  50.7 0.9 collective-permute-start.19
  51.6 3.4 %collective-permute-start.20 = (bf16[3,64,512]{2,1,0:T(8,128)(2,1)S(1)}, bf16[3,64,512]{2,1,0:T(8,128)(2,1)S(1)}, u32[]{:S(2)}, u32[]{:S(2)}) collective-permute-start(bf16[3,64,512]{2,1,0:T(8,128)(2,1)S(1)} %get-tuple-element.39.refs_4_), channel_id=1, source_target_pairs={{0,16},{4,20},{2,18},{6,22},{1,17},{5,21},{3,19},{7,23},{8,24},{12... | collective-permute-start | bytes 589832 | tf_op jit(solution)/shard_map/ppermute | solution.py:74
  55.0 1.9 %collective-permute-start.21 = (bf16[3,64,512]{2,1,0:T(8,128)(2,1)S(1)}, bf16[3,64,512]{2,1,0:T(8,128)(2,1)S(1)}, u32[]{:S(2)}, u32[]{:S(2)}) collective-permute-start(bf16[3,64,512]{2,1,0:T(8,128)(2,1)S(1)} %get-tuple-element.39.refs_4_), channel_id=1, source_target_pairs={{0,24},{4,28},{2,26},{6,30},{1,25},{5,29},{3,27},{7,31},{8,0},{12,... | collective-permute-start | bytes 589832 | tf_op jit(solution)/shard_map/ppermute | solution.py:74
  57.0 2.7 %collective-permute-start.3 = (bf16[128,512]{1,0:T(8,128)(2,1)S(1)}, bf16[128,512]{1,0:T(8,128)(2,1)S(1)}, u32[]{:S(2)}, u32[]{:S(2)}) collective-permute-start(bf16[128,512]{1,0:T(8,128)(2,1)S(1)} %get-tuple-element.31), channel_id=1, source_target_pairs={{0,6},{1,0},{2,4},{3,2},{4,7},{5,1},{6,5},{7,3},{8,14},{9,8},{10,1... | collective-permute-start | bytes 393224 | tf_op jit(solution)/shard_map/ppermute | solution.py:74
  59.7 0.0 collective-permute-done.2.refs_2_
  59.7 0.7 collective-permute-start.30
  60.3 2.8 %collective-permute-done.3.refs_3_ = bf16[128,512]{1,0:T(8,128)(2,1)S(1)} collective-permute-done((bf16[128,512]{1,0:T(8,128)(2,1)S(1)}, bf16[128,512]{1,0:T(8,128)(2,1)S(1)}, u32[]{:S(2)}, u32[]{:S(2)}) %collective-permute-start.3) | collective-permute-done | bytes 131104 | tf_op jit(solution)/shard_map/ppermute | solution.py:74
  63.2 0.0 collective-permute-start.22
  63.2 0.0 collective-permute-done.19.refs_5_
  63.2 0.5 collective-permute-start.23
  63.7 9.1 %collective-permute-done.20.refs_6_ = bf16[3,64,512]{2,1,0:T(8,128)(2,1)S(1)} collective-permute-done((bf16[3,64,512]{2,1,0:T(8,128)(2,1)S(1)}, bf16[3,64,512]{2,1,0:T(8,128)(2,1)S(1)}, u32[]{:S(2)}, u32[]{:S(2)}) %collective-permute-start.20) | collective-permute-done | bytes 196640 | tf_op jit(solution)/shard_map/ppermute | solution.py:74
  72.7 0.0 collective-permute-done.21.refs_7_
  72.8 0.5 collective-permute-start.25
  73.3 2.3 %shard_map.163.view_ref = bf16[4,128,512]{2,1,0:T(8,128)(2,1)S(1)} custom-call(f32[1,2048]{1,0:T(1,128)S(1)} %bitcast.5, bf16[336,512]{1,0:T(8,128)(2,1)S(1)} %collective-permute-done.refs_0_.q_ref, bf16[128,512]{1,0:T(8,128)(2,1)S(1)} %collective-permute-done.1.refs_1_, bf16[128,512]{1,0:T(8,128)(2,1)S(1)} %collective-permute-done.2.refs_2_, ...), custom_call_target="tpu_custom_call" | custom-call | tf_op jit(solution)/shard_map/pallas_call | solution.py:27
  75.6 0.0 collective-permute-done.22.refs_8_
  75.6 0.0 collective-permute-done.25.refs_11_
  75.6 3.9 %shard_map.167 = (bf16[320,512]{1,0:T(8,128)(2,1)S(1)}, bf16[128,512]{1,0:T(8,128)(2,1)S(1)}, bf16[128,512]{1,0:T(8,128)(2,1)S(1)}, bf16[128,512]{1,0:T(8,128)(2,1)S(1)}) custom-call(f32[1,2048]{1,0:T(1,128)S(1)} %bitcast.6, bf16[4,128,512]{2,1,0:T(8,128)(2,1)S(1)} %shard_map.163.view_ref, bf16[3,512,512]{2,1,0:T(8,128)(2,1)S(1)} %get-tuple-element.32.w_ref, ...), custom_call_target="tpu_custom_call" | custom-call | tf_op jit(solution)/shard_map/pallas_call | solution.py:27
  79.5 0.7 collective-permute-start.26
  80.2 3.4 %collective-permute-start.27 = (bf16[128,512]{1,0:T(8,128)(2,1)S(1)}, bf16[128,512]{1,0:T(8,128)(2,1)S(1)}, u32[]{:S(2)}, u32[]{:S(2)}) collective-permute-start(bf16[128,512]{1,0:T(8,128)(2,1)S(1)} %get-tuple-element.41), channel_id=1, source_target_pairs={{0,3},{4,0},{2,1},{6,2},{1,7},{5,4},{3,5},{7,6},{8,11},{12,8},{10,... | collective-permute-start | bytes 393224 | tf_op jit(solution)/shard_map/ppermute | solution.py:74
  83.6 0.5 collective-permute-start.28
  84.1 0.2 collective-permute-start.29
  84.3 0.8 slice_add_fusion
  85.0 4.4 %collective-permute-done.27.refs_1_ = bf16[128,512]{1,0:T(8,128)(2,1)S(1)} collective-permute-done((bf16[128,512]{1,0:T(8,128)(2,1)S(1)}, bf16[128,512]{1,0:T(8,128)(2,1)S(1)}, u32[]{:S(2)}, u32[]{:S(2)}) %collective-permute-start.27) | collective-permute-done | bytes 131104 | tf_op jit(solution)/shard_map/ppermute | solution.py:74
  89.5 3.8 %collective-permute-done.29.refs_3_ = bf16[128,512]{1,0:T(8,128)(2,1)S(1)} collective-permute-done((bf16[128,512]{1,0:T(8,128)(2,1)S(1)}, bf16[128,512]{1,0:T(8,128)(2,1)S(1)}, u32[]{:S(2)}, u32[]{:S(2)}) %collective-permute-start.29) | collective-permute-done | bytes 131104 | tf_op jit(solution)/shard_map/ppermute | solution.py:74
  93.3 0.9 shard_map.168
  (30 shorter events, 0.2 us)
Async XLA Ops:
  0.6 1.5 %copy-start.8 = (bf16[1,64,512]{2,1,0:T(8,128)(2,1)S(1)}, bf16[1,64,512]{2,1,0:T(8,128)(2,1)}, u32[]{:S(2)}) copy-start(bf16[1,64,512]{2,1,0:T(8,128)(2,1)} %param.16) | copy-start | bytes 196612
  0.6 1.5 %copy-start.7 = (bf16[1,64,512]{2,1,0:T(8,128)(2,1)S(1)}, bf16[1,64,512]{2,1,0:T(8,128)(2,1)}, u32[]{:S(2)}) copy-start(bf16[1,64,512]{2,1,0:T(8,128)(2,1)} %param.17) | copy-start | bytes 196612
  0.7 1.5 %copy-start.6 = (bf16[1,64,512]{2,1,0:T(8,128)(2,1)S(1)}, bf16[1,64,512]{2,1,0:T(8,128)(2,1)}, u32[]{:S(2)}) copy-start(bf16[1,64,512]{2,1,0:T(8,128)(2,1)} %param.18) | copy-start | bytes 196612
  2.2 7.7 %collective-permute-start.4 = (bf16[448,512]{1,0:T(8,128)(2,1)S(1)}, bf16[448,512]{1,0:T(8,128)(2,1)S(1)}, u32[]{:S(2)}, u32[]{:S(2)}) collective-permute-start(bf16[448,512]{1,0:T(8,128)(2,1)S(1)} %pad_add_fusion), channel_id=1, source_target_pairs={{0,0},{1,4},{2,2},{3,6},{4,1},{5,5},{6,3},{7,7},{8,8},{9,12},{10,1... | collective-permute-start | bytes 1376264 | tf_op jit(solution)/shard_map/ppermute | solution.py:74
  2.9 13.4 %collective-permute-start.8 = (bf16[3,64,512]{2,1,0:T(8,128)(2,1)S(1)}, bf16[3,64,512]{2,1,0:T(8,128)(2,1)S(1)}, u32[]{:S(2)}, u32[]{:S(2)}) collective-permute-start(bf16[3,64,512]{2,1,0:T(8,128)(2,1)S(1)} %bitcast.13), channel_id=1, source_target_pairs={{0,8},{1,12},{2,10},{3,14},{4,9},{5,13},{6,11},{7,15},{8,16},{9,20... | collective-permute-start | bytes 589832 | tf_op jit(solution)/shard_map/ppermute | solution.py:74
  3.0 15.1 %collective-permute-start.9 = (bf16[3,64,512]{2,1,0:T(8,128)(2,1)S(1)}, bf16[3,64,512]{2,1,0:T(8,128)(2,1)S(1)}, u32[]{:S(2)}, u32[]{:S(2)}) collective-permute-start(bf16[3,64,512]{2,1,0:T(8,128)(2,1)S(1)} %bitcast.14), channel_id=1, source_target_pairs={{0,16},{1,20},{2,18},{3,22},{4,17},{5,21},{6,19},{7,23},{8,24},{9,... | collective-permute-start | bytes 589832 | tf_op jit(solution)/shard_map/ppermute | solution.py:74
  4.9 20.4 %collective-permute-start.5 = (bf16[256,512]{1,0:T(8,128)(2,1)S(1)}, bf16[256,512]{1,0:T(8,128)(2,1)S(1)}, u32[]{:S(2)}, u32[]{:S(2)}) collective-permute-start(bf16[256,512]{1,0:T(8,128)(2,1)S(1)} %pad_add_fusion.3), channel_id=1, source_target_pairs={{0,4},{1,2},{2,6},{3,0},{4,5},{5,3},{6,7},{7,1},{8,12},{9,10},{10,... | collective-permute-start | bytes 786440 | tf_op jit(solution)/shard_map/ppermute | solution.py:74
  8.3 17.0 %collective-permute-start.6 = (bf16[256,512]{1,0:T(8,128)(2,1)S(1)}, bf16[256,512]{1,0:T(8,128)(2,1)S(1)}, u32[]{:S(2)}, u32[]{:S(2)}) collective-permute-start(bf16[256,512]{1,0:T(8,128)(2,1)S(1)} %pad_add_fusion.2), channel_id=1, source_target_pairs={{0,2},{1,6},{2,0},{3,4},{4,3},{5,7},{6,1},{7,5},{8,10},{9,14},{10,... | collective-permute-start | bytes 786440 | tf_op jit(solution)/shard_map/ppermute | solution.py:74
  9.9 17.4 %collective-permute-start.11 = (bf16[448,512]{1,0:T(8,128)(2,1)S(1)}, bf16[448,512]{1,0:T(8,128)(2,1)S(1)}, u32[]{:S(2)}, u32[]{:S(2)}) collective-permute-start(bf16[448,512]{1,0:T(8,128)(2,1)S(1)} %collective-permute-done.4.refs_4_.refs_0_), channel_id=1, source_target_pairs={{0,1},{4,5},{2,3},{6,7},{1,0},{5,4},{3,2},{7,6},{8,9},{12,13},{10,... | collective-permute-start | bytes 1376264 | tf_op jit(solution)/shard_map/ppermute | solution.py:74
  16.4 8.2 %collective-permute-start.10 = (bf16[3,64,512]{2,1,0:T(8,128)(2,1)S(1)}, bf16[3,64,512]{2,1,0:T(8,128)(2,1)S(1)}, u32[]{:S(2)}, u32[]{:S(2)}) collective-permute-start(bf16[3,64,512]{2,1,0:T(8,128)(2,1)S(1)} %bitcast.15), channel_id=1, source_target_pairs={{0,24},{1,28},{2,26},{3,30},{4,25},{5,29},{6,27},{7,31},{8,0},{9,4... | collective-permute-start | bytes 589832 | tf_op jit(solution)/shard_map/ppermute | solution.py:74
  18.1 12.0 %copy-start = (f32[1,64,512]{2,1,0:T(8,128)S(1)}, f32[1,64,512]{2,1,0:T(8,128)}, u32[]{:S(2)}) copy-start(f32[1,64,512]{2,1,0:T(8,128)} %refs_0_.1) | copy-start | bytes 393220
  18.1 12.0 %copy-start.1 = (f32[1,64,512]{2,1,0:T(8,128)S(1)}, f32[1,64,512]{2,1,0:T(8,128)}, u32[]{:S(2)}) copy-start(f32[1,64,512]{2,1,0:T(8,128)} %refs_1_.1) | copy-start | bytes 393220
  18.1 12.0 %copy-start.2 = (f32[1,64,512]{2,1,0:T(8,128)S(1)}, f32[1,64,512]{2,1,0:T(8,128)}, u32[]{:S(2)}) copy-start(f32[1,64,512]{2,1,0:T(8,128)} %refs_2_.1) | copy-start | bytes 393220
  18.1 12.0 %copy-start.3 = (bf16[128,2048]{1,0:T(8,128)(2,1)S(1)}, bf16[128,2048]{1,0:T(8,128)(2,1)}, u32[]{:S(2)}) copy-start(bf16[128,2048]{1,0:T(8,128)(2,1)} %q_ref.1) | copy-start | bytes 1572868
  18.1 12.0 %copy-start.5 = (s32[1,4]{1,0:T(1,128)S(1)}, s32[1,4]{1,0:T(1,128)}, u32[]{:S(2)}) copy-start(s32[1,4]{1,0:T(1,128)} %len_ref.1) | copy-start | bytes 52
  18.1 9.2 %collective-permute-start.7 = (bf16[256,512]{1,0:T(8,128)(2,1)S(1)}, bf16[256,512]{1,0:T(8,128)(2,1)S(1)}, u32[]{:S(2)}, u32[]{:S(2)}) collective-permute-start(bf16[256,512]{1,0:T(8,128)(2,1)S(1)} %pad_add_fusion.1), channel_id=1, source_target_pairs={{0,6},{1,0},{2,4},{3,2},{4,7},{5,1},{6,5},{7,3},{8,14},{9,8},{10,1... | collective-permute-start | bytes 786440 | tf_op jit(solution)/shard_map/ppermute | solution.py:74
  24.5 2.8 %collective-permute-start.12 = (bf16[3,64,512]{2,1,0:T(8,128)(2,1)S(1)}, bf16[3,64,512]{2,1,0:T(8,128)(2,1)S(1)}, u32[]{:S(2)}, u32[]{:S(2)}) collective-permute-start(bf16[3,64,512]{2,1,0:T(8,128)(2,1)S(1)} %collective-permute-done.8.refs_4_), channel_id=1, source_target_pairs={{0,1},{4,5},{2,3},{6,7},{1,0},{5,4},{3,2},{7,6},{8,9},{12,13},{10,... | collective-permute-start | bytes 589832 | tf_op jit(solution)/shard_map/ppermute | solution.py:74
  25.3 2.0 %collective-permute-start.13 = (bf16[3,64,512]{2,1,0:T(8,128)(2,1)S(1)}, bf16[3,64,512]{2,1,0:T(8,128)(2,1)S(1)}, u32[]{:S(2)}, u32[]{:S(2)}) collective-permute-start(bf16[3,64,512]{2,1,0:T(8,128)(2,1)S(1)} %collective-permute-done.9.refs_5_), channel_id=1, source_target_pairs={{0,1},{4,5},{2,3},{6,7},{1,0},{5,4},{3,2},{7,6},{8,9},{12,13},{10,... | collective-permute-start | bytes 589832 | tf_op jit(solution)/shard_map/ppermute | solution.py:74
  25.3 2.0 %collective-permute-start.14 = (bf16[3,64,512]{2,1,0:T(8,128)(2,1)S(1)}, bf16[3,64,512]{2,1,0:T(8,128)(2,1)S(1)}, u32[]{:S(2)}, u32[]{:S(2)}) collective-permute-start(bf16[3,64,512]{2,1,0:T(8,128)(2,1)S(1)} %collective-permute-done.10.refs_6_), channel_id=1, source_target_pairs={{0,1},{4,5},{2,3},{6,7},{1,0},{5,4},{3,2},{7,6},{8,9},{12,13},{10,... | collective-permute-start | bytes 589832 | tf_op jit(solution)/shard_map/ppermute | solution.py:74
  29.9 2.4 %collective-permute-start.15 = (bf16[4,3,64,512]{3,2,1,0:T(8,128)(2,1)S(1)}, bf16[4,3,64,512]{3,2,1,0:T(8,128)(2,1)S(1)}, u32[]{:S(2)}, u32[]{:S(2)}) collective-permute-start(bf16[4,3,64,512]{3,2,1,0:T(8,128)(2,1)S(1)} %get-tuple-element.34), channel_id=1, source_target_pairs={{0,1},{4,5},{2,3},{6,7},{1,0},{5,4},{3,2},{7,6},{8,9},{12,13},{10,... | collective-permute-start | bytes 2359304 | tf_op jit(solution)/shard_map/ppermute | solution.py:74
  30.7 7.5 %collective-permute-start = (bf16[336,512]{1,0:T(8,128)(2,1)S(1)}, bf16[336,512]{1,0:T(8,128)(2,1)S(1)}, u32[]{:S(2)}, u32[]{:S(2)}) collective-permute-start(bf16[336,512]{1,0:T(8,128)(2,1)S(1)} %get-tuple-element.28), channel_id=1, source_target_pairs={{0,0},{1,4},{2,2},{3,6},{4,1},{5,5},{6,3},{7,7},{8,8},{9,12},{10,1... | collective-permute-start | bytes 1032200 | tf_op jit(solution)/shard_map/ppermute | solution.py:74
  32.3 41.0 %copy-start.4 = (f32[2048]{0:T(1024)S(1)}, f32[2048]{0:T(1024)}, u32[]{:S(2)}) copy-start(f32[2048]{0:T(1024)} %param.15) | copy-start | bytes 24580
  32.5 7.2 %collective-permute-start.16 = (bf16[3,64,512]{2,1,0:T(8,128)(2,1)S(1)}, bf16[3,64,512]{2,1,0:T(8,128)(2,1)S(1)}, u32[]{:S(2)}, u32[]{:S(2)}) collective-permute-start(bf16[3,64,512]{2,1,0:T(8,128)(2,1)S(1)} %get-tuple-element.36), channel_id=1, source_target_pairs={{0,8},{4,12},{2,10},{6,14},{1,9},{5,13},{3,11},{7,15},{8,16},{12,2... | collective-permute-start | bytes 589832 | tf_op jit(solution)/shard_map/ppermute | solution.py:74
  33.5 17.1 %collective-permute-start.17 = (bf16[3,64,512]{2,1,0:T(8,128)(2,1)S(1)}, bf16[3,64,512]{2,1,0:T(8,128)(2,1)S(1)}, u32[]{:S(2)}, u32[]{:S(2)}) collective-permute-start(bf16[3,64,512]{2,1,0:T(8,128)(2,1)S(1)} %get-tuple-element.37), channel_id=1, source_target_pairs={{0,16},{4,20},{2,18},{6,22},{1,17},{5,21},{3,19},{7,23},{8,24},{12... | collective-permute-start | bytes 589832 | tf_op jit(solution)/shard_map/ppermute | solution.py:74
  33.9 16.7 %collective-permute-start.18 = (bf16[3,64,512]{2,1,0:T(8,128)(2,1)S(1)}, bf16[3,64,512]{2,1,0:T(8,128)(2,1)S(1)}, u32[]{:S(2)}, u32[]{:S(2)}) collective-permute-start(bf16[3,64,512]{2,1,0:T(8,128)(2,1)S(1)} %get-tuple-element.38), channel_id=1, source_target_pairs={{0,24},{4,28},{2,26},{6,30},{1,25},{5,29},{3,27},{7,31},{8,0},{12,... | collective-permute-start | bytes 589832 | tf_op jit(solution)/shard_map/ppermute | solution.py:74
  35.8 21.2 %collective-permute-start.1 = (bf16[128,512]{1,0:T(8,128)(2,1)S(1)}, bf16[128,512]{1,0:T(8,128)(2,1)S(1)}, u32[]{:S(2)}, u32[]{:S(2)}) collective-permute-start(bf16[128,512]{1,0:T(8,128)(2,1)S(1)} %get-tuple-element.29), channel_id=1, source_target_pairs={{0,4},{1,2},{2,6},{3,0},{4,5},{5,3},{6,7},{7,1},{8,12},{9,10},{10,... | collective-permute-start | bytes 393224 | tf_op jit(solution)/shard_map/ppermute | solution.py:74
  38.2 21.5 %collective-permute-start.2 = (bf16[128,512]{1,0:T(8,128)(2,1)S(1)}, bf16[128,512]{1,0:T(8,128)(2,1)S(1)}, u32[]{:S(2)}, u32[]{:S(2)}) collective-permute-start(bf16[128,512]{1,0:T(8,128)(2,1)S(1)} %get-tuple-element.30), channel_id=1, source_target_pairs={{0,2},{1,6},{2,0},{3,4},{4,3},{5,7},{6,1},{7,5},{8,10},{9,14},{10,... | collective-permute-start | bytes 393224 | tf_op jit(solution)/shard_map/ppermute | solution.py:74
  50.7 12.5 %collective-permute-start.19 = (bf16[3,64,512]{2,1,0:T(8,128)(2,1)S(1)}, bf16[3,64,512]{2,1,0:T(8,128)(2,1)S(1)}, u32[]{:S(2)}, u32[]{:S(2)}) collective-permute-start(bf16[3,64,512]{2,1,0:T(8,128)(2,1)S(1)} %get-tuple-element.39.refs_4_), channel_id=1, source_target_pairs={{0,8},{4,12},{2,10},{6,14},{1,9},{5,13},{3,11},{7,15},{8,16},{12,2... | collective-permute-start | bytes 589832 | tf_op jit(solution)/shard_map/ppermute | solution.py:74
  51.6 21.1 %collective-permute-start.20 = (bf16[3,64,512]{2,1,0:T(8,128)(2,1)S(1)}, bf16[3,64,512]{2,1,0:T(8,128)(2,1)S(1)}, u32[]{:S(2)}, u32[]{:S(2)}) collective-permute-start(bf16[3,64,512]{2,1,0:T(8,128)(2,1)S(1)} %get-tuple-element.39.refs_4_), channel_id=1, source_target_pairs={{0,16},{4,20},{2,18},{6,22},{1,17},{5,21},{3,19},{7,23},{8,24},{12... | collective-permute-start | bytes 589832 | tf_op jit(solution)/shard_map/ppermute | solution.py:74
  55.0 17.7 %collective-permute-start.21 = (bf16[3,64,512]{2,1,0:T(8,128)(2,1)S(1)}, bf16[3,64,512]{2,1,0:T(8,128)(2,1)S(1)}, u32[]{:S(2)}, u32[]{:S(2)}) collective-permute-start(bf16[3,64,512]{2,1,0:T(8,128)(2,1)S(1)} %get-tuple-element.39.refs_4_), channel_id=1, source_target_pairs={{0,24},{4,28},{2,26},{6,30},{1,25},{5,29},{3,27},{7,31},{8,0},{12,... | collective-permute-start | bytes 589832 | tf_op jit(solution)/shard_map/ppermute | solution.py:74
  57.0 6.2 %collective-permute-start.3 = (bf16[128,512]{1,0:T(8,128)(2,1)S(1)}, bf16[128,512]{1,0:T(8,128)(2,1)S(1)}, u32[]{:S(2)}, u32[]{:S(2)}) collective-permute-start(bf16[128,512]{1,0:T(8,128)(2,1)S(1)} %get-tuple-element.31), channel_id=1, source_target_pairs={{0,6},{1,0},{2,4},{3,2},{4,7},{5,1},{6,5},{7,3},{8,14},{9,8},{10,1... | collective-permute-start | bytes 393224 | tf_op jit(solution)/shard_map/ppermute | solution.py:74
  59.7 24.6 %collective-permute-start.30 = (f32[3,64,512]{2,1,0:T(8,128)S(1)}, f32[3,64,512]{2,1,0:T(8,128)S(1)}, u32[]{:S(2)}, u32[]{:S(2)}) collective-permute-start(f32[3,64,512]{2,1,0:T(8,128)S(1)} %get-tuple-element.48), channel_id=1, source_target_pairs={{0,0},{4,1},{2,2},{6,3},{1,4},{5,5},{3,6},{7,7},{8,8},{12,9},{10,1... | collective-permute-start | bytes 1179656 | tf_op jit(solution)/shard_map/ppermute | solution.py:74
  63.2 12.4 %collective-permute-start.22 = (bf16[3,64,512]{2,1,0:T(8,128)(2,1)S(1)}, bf16[3,64,512]{2,1,0:T(8,128)(2,1)S(1)}, u32[]{:S(2)}, u32[]{:S(2)}) collective-permute-start(bf16[3,64,512]{2,1,0:T(8,128)(2,1)S(1)} %get-tuple-element.39.refs_4_), channel_id=1, source_target_pairs={{0,1},{4,5},{2,3},{6,7},{1,0},{5,4},{3,2},{7,6},{8,9},{12,13},{10,... | collective-permute-start | bytes 589832 | tf_op jit(solution)/shard_map/ppermute | solution.py:74
  63.2 12.4 %collective-permute-start.23 = (bf16[3,64,512]{2,1,0:T(8,128)(2,1)S(1)}, bf16[3,64,512]{2,1,0:T(8,128)(2,1)S(1)}, u32[]{:S(2)}, u32[]{:S(2)}) collective-permute-start(bf16[3,64,512]{2,1,0:T(8,128)(2,1)S(1)} %collective-permute-done.19.refs_5_), channel_id=1, source_target_pairs={{0,1},{4,5},{2,3},{6,7},{1,0},{5,4},{3,2},{7,6},{8,9},{12,13},{10,... | collective-permute-start | bytes 589832 | tf_op jit(solution)/shard_map/ppermute | solution.py:74
  72.7 2.8 %collective-permute-start.24 = (bf16[3,64,512]{2,1,0:T(8,128)(2,1)S(1)}, bf16[3,64,512]{2,1,0:T(8,128)(2,1)S(1)}, u32[]{:S(2)}, u32[]{:S(2)}) collective-permute-start(bf16[3,64,512]{2,1,0:T(8,128)(2,1)S(1)} %collective-permute-done.20.refs_6_), channel_id=1, source_target_pairs={{0,1},{4,5},{2,3},{6,7},{1,0},{5,4},{3,2},{7,6},{8,9},{12,13},{10,... | collective-permute-start | bytes 589832 | tf_op jit(solution)/shard_map/ppermute | solution.py:74
  72.8 2.8 %collective-permute-start.25 = (bf16[3,64,512]{2,1,0:T(8,128)(2,1)S(1)}, bf16[3,64,512]{2,1,0:T(8,128)(2,1)S(1)}, u32[]{:S(2)}, u32[]{:S(2)}) collective-permute-start(bf16[3,64,512]{2,1,0:T(8,128)(2,1)S(1)} %collective-permute-done.21.refs_7_), channel_id=1, source_target_pairs={{0,1},{4,5},{2,3},{6,7},{1,0},{5,4},{3,2},{7,6},{8,9},{12,13},{10,... | collective-permute-start | bytes 589832 | tf_op jit(solution)/shard_map/ppermute | solution.py:74
  79.5 13.8 %collective-permute-start.26 = (bf16[320,512]{1,0:T(8,128)(2,1)S(1)}, bf16[320,512]{1,0:T(8,128)(2,1)S(1)}, u32[]{:S(2)}, u32[]{:S(2)}) collective-permute-start(bf16[320,512]{1,0:T(8,128)(2,1)S(1)} %get-tuple-element.40), channel_id=1, source_target_pairs={{0,0},{4,1},{2,2},{6,3},{1,4},{5,5},{3,6},{7,7},{8,8},{12,9},{10,1... | collective-permute-start | bytes 983048 | tf_op jit(solution)/shard_map/ppermute | solution.py:74
  80.2 9.3 %collective-permute-start.27 = (bf16[128,512]{1,0:T(8,128)(2,1)S(1)}, bf16[128,512]{1,0:T(8,128)(2,1)S(1)}, u32[]{:S(2)}, u32[]{:S(2)}) collective-permute-start(bf16[128,512]{1,0:T(8,128)(2,1)S(1)} %get-tuple-element.41), channel_id=1, source_target_pairs={{0,3},{4,0},{2,1},{6,2},{1,7},{5,4},{3,5},{7,6},{8,11},{12,8},{10,... | collective-permute-start | bytes 393224 | tf_op jit(solution)/shard_map/ppermute | solution.py:74
  83.6 5.9 %collective-permute-start.28 = (bf16[128,512]{1,0:T(8,128)(2,1)S(1)}, bf16[128,512]{1,0:T(8,128)(2,1)S(1)}, u32[]{:S(2)}, u32[]{:S(2)}) collective-permute-start(bf16[128,512]{1,0:T(8,128)(2,1)S(1)} %get-tuple-element.42), channel_id=1, source_target_pairs={{0,2},{4,3},{2,0},{6,1},{1,6},{5,7},{3,4},{7,5},{8,10},{12,11},{10... | collective-permute-start | bytes 393224 | tf_op jit(solution)/shard_map/ppermute | solution.py:74
  84.1 9.2 %collective-permute-start.29 = (bf16[128,512]{1,0:T(8,128)(2,1)S(1)}, bf16[128,512]{1,0:T(8,128)(2,1)S(1)}, u32[]{:S(2)}, u32[]{:S(2)}) collective-permute-start(bf16[128,512]{1,0:T(8,128)(2,1)S(1)} %get-tuple-element.43), channel_id=1, source_target_pairs={{0,1},{4,2},{2,3},{6,0},{1,5},{5,6},{3,7},{7,4},{8,9},{12,10},{10,... | collective-permute-start | bytes 393224 | tf_op jit(solution)/shard_map/ppermute | solution.py:74
